TPU v7x, 32 devices: a whole 2x2x4 slice. The times are simulated.
32 devices in a mesh: pairs: 16 (over z, y, x), comp: 2 (over core).
Axes of the slice: x: 2, y: 2, z: 4, core: 2. Of those that a mesh axis runs over, the one named last changes fastest.
Arguments:
- effects: float32 [49, 131072], P(None, 'pairs'), may hold values from -24 to 24
- se_table: float32 [16, 49], replicated, may hold values from 0.5 to 2
- se_index: int32 [256], P('pairs'), may hold values from 0 to 15
- base_root: float32 [16, 49, 49], replicated, may hold values from -0.875 to 0.875
- grid_scale: float32 [16], replicated, may hold values from 0.25 to 4
- comp_base: int32 [256], P('comp'), may hold values from 0 to 15
- comp_grid: int32 [256], P('comp'), may hold values from 0 to 15
- weights: float32 [256], P('comp'), may hold values from 0.2 to 5
Outputs:
- responsibility: float32 [256, 131072], P('comp', 'pairs')
- log_weights: float32 [256], P('comp')
- pair_loglik: float32 [131072], P('pairs')
All inputs are finite; a program needn't handle non-finite values.
Results may differ from a plain program's by a relative error of at most 0.0003.
Values sent between devices are 32-bit elements; how exact they have to be, the bound alone decides.
A program may use at most 384 MiB of HBM per device.

v0:
```python
import math

import jax
import jax.numpy as jnp
from jax import lax
from jax.experimental import pallas as pl
from jax.experimental.pallas import tpu as pltpu
from jax.sharding import PartitionSpec as P

SUB = 8
GROUP = 4
CHUNKS = 8
VMEM_GRANT = 58 * 1024 * 1024
MESH = pl.DeviceIdType.MESH


def split_terms(value):
    high = value.astype(jnp.bfloat16)
    return high, (value - high.astype(jnp.float32)).astype(jnp.bfloat16)


def put_row(table, row, inv):
    slot = table.shape[1] // 4
    comps = table.shape[2] // 2
    if len(inv) % 2:
        inv = inv + [jnp.zeros((SUB, comps), jnp.float32)]
    high, low = split_terms(jnp.concatenate(inv, axis=0))
    lanes = slice((row % 2) * comps, (row % 2 + 1) * comps)
    height = len(inv) * SUB
    table[row // 2, 0:height, lanes] = high
    table[row // 2, slot : slot + height, lanes] = high
    table[row // 2, 2 * slot : 2 * slot + height, lanes] = low
    table[row // 2, 3 * slot : 3 * slot + height, lanes] = low


def factor_steps(pattern, se_table, covar, prior, upper, inverse, edge, pivots, table, bias, tissues):
    constant = 0.5 * tissues * math.log(2.0 * math.pi)
    comps = covar.shape[2]
    border = tissues % SUB == 1
    core = tissues - 1 if border else tissues
    blocks = -(-core // SUB)
    sub_iota = lax.broadcasted_iota(jnp.int32, (SUB, comps), 0)
    for first in range(0, core, GROUP):
        row_block = first // SUB
        rows = range(first, min(first + GROUP, core))
        system, solved = {}, {}
        for row in rows:
            system[row] = [covar[row, v * SUB : (v + 1) * SUB, :] for v in range(row_block, blocks)]
            on_diag = sub_iota == row % SUB
            deviation = se_table[pattern, row]
            system[row][0] = system[row][0] + jnp.where(on_diag, deviation * deviation, 0.0)
            solved[row] = [jnp.zeros((SUB, comps), jnp.float32) for _ in range(row_block)]
            solved[row].append(jnp.where(on_diag, 1.0, 0.0))
        for col in range(first):
            col_block = col // SUB
            up = [upper[col, v * SUB : (v + 1) * SUB, :] for v in range(row_block, blocks)]
            inv = [inverse[col, v * SUB : (v + 1) * SUB, :] for v in range(col_block + 1)]
            for row in rows:
                mult = upper[col, row : row + 1, :]
                for n, part in enumerate(up):
                    system[row][n] = system[row][n] - mult * part
                for n, part in enumerate(inv):
                    solved[row][n] = solved[row][n] - mult * part
        for row in rows:
            pivot = system[row][0][row % SUB : row % SUB + 1, :]
            root = lax.rsqrt(pivot)
            pivots[row : row + 1, :] = pivot
            up = [part * root for part in system[row]]
            inv = [part * root for part in solved[row]]
            for n, part in enumerate(up):
                upper[row, (row_block + n) * SUB : (row_block + n + 1) * SUB, :] = part
            for n, part in enumerate(inv):
                inverse[row, n * SUB : (n + 1) * SUB, :] = part
            for later in rows:
                if later > row:
                    mult = up[0][later % SUB : later % SUB + 1, :]
                    for n, part in enumerate(up):
                        system[later][n] = system[later][n] - mult * part
                    for n, part in enumerate(inv):
                        solved[later][n] = solved[later][n] - mult * part
            put_row(table, row, inv)
            if border:
                terms = [part * covar[core, n * SUB : (n + 1) * SUB, :] for n, part in enumerate(inv)]
                edge[row * SUB : (row + 1) * SUB, :] = sum(terms)
        yield
    if border:
        deviation = se_table[pattern, core]
        pivot = covar[core, core : core + 1, :] + deviation * deviation
        solved = [jnp.zeros((SUB, comps), jnp.float32) for _ in range(blocks)]
        for block in range(blocks):
            lines = [edge[pl.ds(block * SUB * SUB + n, SUB, stride=SUB), :] for n in range(SUB)]
            edge[core * SUB + block * SUB : core * SUB + (block + 1) * SUB, :] = sum(lines)
        for col in range(core):
            mult = edge[core * SUB + col : core * SUB + col + 1, :]
            pivot = pivot - mult * mult
            for n in range(col // SUB + 1):
                solved[n] = solved[n] - mult * inverse[col, n * SUB : (n + 1) * SUB, :]
        root = lax.rsqrt(pivot)
        pivots[core : core + 1, :] = pivot
        solved.append(jnp.where(sub_iota == core % SUB, 1.0, 0.0))
        put_row(table, core, [part * root for part in solved])
        yield
    logdet = jnp.sum(jnp.log(pivots[...]), axis=0, keepdims=True)
    bias[...] = jnp.log(prior[...]) - 0.5 * logdet - constant


def pack_tile(tile, effects, wide, ready):
    tissues = effects.shape[0]
    slot = wide.shape[0] // 2
    width = wide.shape[1]
    values = effects[:, pl.ds(pl.multiple_of(tile * width, width), width)]
    high = values.astype(jnp.bfloat16).astype(jnp.float32)
    wide[0:tissues, :] = high
    wide[slot : slot + tissues, :] = values - high
    ready[...] = wide[...].T.astype(jnp.bfloat16)


def finish_tile(tile, found, scaled, peak, total):
    width = found.shape[0]
    columns = pl.ds(pl.multiple_of(tile * width, width), width)
    values = found[...].T
    top = jnp.max(values, axis=0, keepdims=True)
    shifted = jnp.exp(values - top)
    scaled[:, columns] = shifted
    peak[:, columns] = top
    total[:, columns] = jnp.sum(shifted, axis=0, keepdims=True)


def score_steps(tissues, packed, table, bias, quad, found):
    comps = table.shape[2] // 2
    both = jnp.concatenate([packed[...], packed[...]], axis=1)
    last = table.shape[0] - 1
    for index in range(last + 1):
        if 2 * index + 1 < tissues:
            white = jnp.dot(both, table[index], preferred_element_type=jnp.float32)
            white = white * white
            part = white[:, :comps] + white[:, comps:]
        else:
            white = jnp.dot(both, table[index, :, :comps], preferred_element_type=jnp.float32)
            part = white * white
        if index == 0:
            quad[...] = part
        elif index < last:
            quad[...] += part
        else:
            found[...] = bias[...] - 0.5 * (quad[...] + part)
        if index % (GROUP // 2) == GROUP // 2 - 1:
            yield


def spread_covariances(roots, grid_scale, comp_base, comp_grid, stack, covar):
    tissues, bases = roots.shape[0], roots.shape[1]
    comps = covar.shape[2]
    for base in range(bases):
        root = roots[:, base, :]
        stack[:, base, :] = lax.dot_general(
            root, root, (((1,), (1,)), ((), ())),
            precision=lax.Precision.HIGHEST, preferred_element_type=jnp.float32,
        )
    pick = (lax.broadcasted_iota(jnp.int32, (bases, comps), 0) == comp_base[...]).astype(jnp.float32)
    pick = jnp.concatenate([pick, pick, pick], axis=0).astype(jnp.bfloat16)
    scale = jnp.zeros((1, comps), jnp.float32)
    for grid in range(grid_scale.shape[0]):
        scale = jnp.where(comp_grid[...] == grid, grid_scale[grid], scale)
    scale = scale * scale
    for row in range(tissues):
        value = stack[row]
        high = value.astype(jnp.bfloat16).astype(jnp.float32)
        rest = value - high
        middle = rest.astype(jnp.bfloat16).astype(jnp.float32)
        terms = jnp.concatenate([high, middle, rest - middle], axis=0).astype(jnp.bfloat16)
        spread = lax.dot_general(
            terms, pick, (((0,), (0,)), ((), ())), preferred_element_type=jnp.float32
        )
        covar[row, 0:tissues, :] = spread * scale


def score_body(index_hbm, se_hbm, grid_hbm, effects_hbm, roots_hbm, base_hbm, comp_grid_hbm, prior_hbm,
               scaled_hbm, peak_hbm, total_hbm, scaled, peak, total, sent,
               se_index, se_table, grid_scale, effects, roots, comp_base, comp_grid, prior, arrived,
               order, stack, covar, upper, inverse, edge, pivots, table, bias, quad, found, wide, packed, ready):
    tissues = effects.shape[0]
    tiles = se_index.shape[0]
    copies = [
        pltpu.make_async_copy(source, target, arrived.at[n])
        for n, (source, target) in enumerate((
            (roots_hbm, roots), (base_hbm, comp_base), (comp_grid_hbm, comp_grid), (grid_hbm, grid_scale),
            (index_hbm, se_index), (se_hbm, se_table), (prior_hbm, prior), (effects_hbm, effects),
        ))
    ]
    for copy in copies:
        copy.start()
    table[...] = jnp.zeros(table.shape, table.dtype)
    wide[...] = jnp.zeros(wide.shape, wide.dtype)
    pivots[...] = jnp.ones(pivots.shape, pivots.dtype)
    found[...] = jnp.zeros(found.shape, found.dtype)
    for copy in copies[:-1]:
        copy.wait()
    keys = [se_index[t] * tiles + t for t in range(tiles)]
    for t in range(tiles):
        rank = sum((keys[other] < keys[t]).astype(jnp.int32) for other in range(tiles) if other != t)
        order[rank] = t
    spread_covariances(roots, grid_scale, comp_base, comp_grid, stack, covar)
    copies[-1].wait()

    def leave(step):
        width = found.shape[0]
        columns = pl.ds(pl.multiple_of(order[step] * width, width), width)
        return pltpu.make_async_copy(scaled.at[:, columns], scaled_hbm.at[:, columns], sent.at[step])

    def factoring(pattern):
        return factor_steps(pattern, se_table, covar, prior, upper, inverse, edge, pivots, table, bias, tissues)

    def one_tile(step, steps):
        finish_tile(order[jnp.maximum(step - 1, 0)], found, scaled, peak, total)
        scores = score_steps(tissues, packed, table, bias, quad, found)
        for count in range(-(-tissues // GROUP)):
            next(scores, None)
            next(steps, None)
            if count == 2:
                pack_tile(order[jnp.minimum(step + 1, tiles - 1)], effects, wide, ready)
        for _ in scores:
            pass
        for _ in steps:
            pass
        packed[...] = ready[...]

    pack_tile(order[0], effects, wide, packed)
    for _ in factoring(se_index[order[0]]):
        pass

    @pl.loop(0, tiles)
    def _(step):
        later = se_index[order[jnp.minimum(step + 1, tiles - 1)]]
        fresh = se_index[order[step]] != later

        @pl.when(fresh)
        def _():
            one_tile(step, factoring(later))

        @pl.when(jnp.logical_not(fresh))
        def _():
            one_tile(step, iter(()))

        @pl.when(step > 0)
        def _():
            leave(step - 1).start()

    finish_tile(order[tiles - 1], found, scaled, peak, total)
    last = [
        leave(tiles - 1),
        pltpu.make_async_copy(peak, peak_hbm, sent.at[tiles]),
        pltpu.make_async_copy(total, total_hbm, sent.at[tiles + 1]),
    ]
    for copy in last:
        copy.start()

    @pl.loop(0, tiles - 1)
    def _(step):
        leave(step).wait()

    for copy in last:
        copy.wait()


def score_tiles(effects, se_table, se_index, base_root, grid_scale, comp_base, comp_grid, weights):
    tissues, pairs = effects.shape
    bases = base_root.shape[0]
    tiles = se_index.shape[0]
    comps = weights.shape[0]
    width = pairs // tiles
    padded = SUB * (-(-tissues // SUB))
    slot = 16 * (-(-tissues // 16))
    hbm = pl.BlockSpec(memory_space=pltpu.HBM)
    return pl.pallas_call(
        score_body,
        in_specs=[hbm] * 8,
        out_specs=[hbm] * 3,
        scratch_shapes=[
            pltpu.VMEM((comps, pairs), jnp.float32),
            pltpu.VMEM((1, pairs), jnp.float32),
            pltpu.VMEM((1, pairs), jnp.float32),
            pltpu.SemaphoreType.DMA((tiles + 2,)),
            pltpu.SMEM(se_index.shape, jnp.int32),
            pltpu.SMEM(se_table.shape, jnp.float32),
            pltpu.SMEM(grid_scale.shape, jnp.float32),
            pltpu.VMEM(effects.shape, jnp.float32),
            pltpu.VMEM((tissues, bases, tissues), jnp.float32),
            pltpu.VMEM((1, comps), jnp.int32),
            pltpu.VMEM((1, comps), jnp.int32),
            pltpu.VMEM((1, comps), jnp.float32),
            pltpu.SemaphoreType.DMA((8,)),
            pltpu.SMEM((tiles,), jnp.int32),
            pltpu.VMEM((tissues, bases, tissues), jnp.float32),
            pltpu.VMEM((tissues, padded, comps), jnp.float32),
            pltpu.VMEM((tissues, padded, comps), jnp.float32),
            pltpu.VMEM((tissues, padded, comps), jnp.float32),
            pltpu.VMEM(((SUB + 1) * padded, comps), jnp.float32),
            pltpu.VMEM((padded, comps), jnp.float32),
            pltpu.VMEM(((tissues + 1) // 2, 4 * slot, 2 * comps), jnp.bfloat16),
            pltpu.VMEM((1, comps), jnp.float32),
            pltpu.VMEM((width, comps), jnp.float32),
            pltpu.VMEM((width, comps), jnp.float32),
            pltpu.VMEM((2 * slot, width), jnp.float32),
            pltpu.VMEM((width, 2 * slot), jnp.bfloat16),
            pltpu.VMEM((width, 2 * slot), jnp.bfloat16),
        ],
        out_shape=[
            jax.ShapeDtypeStruct((comps, pairs), jnp.float32),
            jax.ShapeDtypeStruct((1, pairs), jnp.float32),
            jax.ShapeDtypeStruct((1, pairs), jnp.float32),
        ],
        compiler_params=pltpu.CompilerParams(vmem_limit_bytes=VMEM_GRANT),
        name="score_tiles",
    )(se_index, se_table, grid_scale, effects, jnp.transpose(base_root, (1, 0, 2)),
      comp_base[None], comp_grid[None], weights[None])


def combine_body(sizes, scaled_hbm, peak_hbm, total_hbm, loglik_hbm, factor_hbm, weights_hbm,
                 scaled, peak, total, loglik, factor, mass, log_weights, peak_there, total_there, gathered,
                 arrived, sent, send_sem, recv_sem, mass_send, mass_recv):
    comps, pairs = scaled.shape
    groups, places = sizes
    width = pairs // CHUNKS
    me_pair, me_comp = lax.axis_index("pairs"), lax.axis_index("comp")
    barrier = pltpu.get_barrier_semaphore()
    partners = [(me_pair, lax.rem(me_comp + hop, groups)) for hop in range(1, groups)]
    peers = [(lax.rem(me_pair + hop, places), me_comp) for hop in range(1, places)]
    for other in peers + partners:
        pl.semaphore_signal(barrier, inc=1, device_id=other, device_id_type=MESH)
    loads = [
        pltpu.make_async_copy(peak_hbm, peak, arrived.at[CHUNKS]),
        pltpu.make_async_copy(total_hbm, total, arrived.at[CHUNKS + 1]),
    ]
    for chunk in range(CHUNKS):
        columns = pl.ds(chunk * width, width)
        loads.append(pltpu.make_async_copy(scaled_hbm.at[:, columns], scaled.at[:, columns], arrived.at[chunk]))
    for copy in loads:
        copy.start()
    for copy in loads[:2]:
        copy.wait()
    pl.semaphore_wait(barrier, groups + places - 2)
    copies = []
    for hop, other in enumerate(partners):
        for n, (own, there) in enumerate(((peak, peak_there), (total, total_there))):
            copies.append(pltpu.make_async_remote_copy(
                src_ref=own, dst_ref=there.at[hop],
                send_sem=send_sem.at[2 * hop + n], recv_sem=recv_sem.at[2 * hop + n],
                device_id=other, device_id_type=MESH,
            ))
    for copy in copies:
        copy.start()
    for copy in loads[2:]:
        copy.wait()
    for copy in copies:
        copy.wait()
    top = peak[...]
    for hop in range(groups - 1):
        top = jnp.maximum(top, peak_there[hop])
    summed = total[...] * jnp.exp(peak[...] - top)
    for hop in range(groups - 1):
        summed = summed + total_there[hop] * jnp.exp(peak_there[hop] - top)
    joint = top + jnp.log(summed)
    loglik[...] = joint
    factor[...] = jnp.exp(peak[...] - joint)

    def add_columns(step, acc):
        columns = pl.ds(pl.multiple_of(step * width, width), width)
        posterior = scaled[:, columns] * factor[:, columns]
        for lane in range(0, width, 128):
            acc = acc + posterior[:, lane : lane + 128]
        return acc

    acc = lax.fori_loop(0, CHUNKS, add_columns, jnp.zeros((comps, 128), jnp.float32))
    mass[...] = jnp.sum(acc.T, axis=0, keepdims=True)
    sends = [
        pltpu.make_async_remote_copy(
            src_ref=mass, dst_ref=gathered.at[hop],
            send_sem=mass_send.at[hop], recv_sem=mass_recv.at[hop],
            device_id=other, device_id_type=MESH,
        )
        for hop, other in enumerate(peers)
    ]
    for copy in sends:
        copy.start()
    leaves = [
        pltpu.make_async_copy(loglik, loglik_hbm, sent.at[0]),
        pltpu.make_async_copy(factor, factor_hbm, sent.at[1]),
        pltpu.make_async_copy(log_weights, weights_hbm, sent.at[2]),
    ]
    for copy in leaves[:2]:
        copy.start()
    for copy in sends:
        copy.wait()
    masses = mass[...]
    for hop in range(places - 1):
        masses = masses + gathered[hop]
    log_weights[...] = jnp.log((masses + 1.0) / (pairs * places + comps * groups))
    leaves[2].start()
    for copy in leaves:
        copy.wait()


def combine(scaled, peak, total):
    comps, pairs = scaled.shape
    groups, places = lax.axis_size("comp"), lax.axis_size("pairs")
    hbm = pl.BlockSpec(memory_space=pltpu.HBM)

    def body(*refs):
        combine_body((groups, places), *refs)

    pair_row, comp_row = (1, pairs), (1, comps)
    return pl.pallas_call(
        body,
        in_specs=[hbm] * 3,
        out_specs=[hbm] * 3,
        out_shape=[
            jax.ShapeDtypeStruct(pair_row, jnp.float32),
            jax.ShapeDtypeStruct(pair_row, jnp.float32),
            jax.ShapeDtypeStruct(comp_row, jnp.float32),
        ],
        scratch_shapes=[
            pltpu.VMEM((comps, pairs), jnp.float32),
            pltpu.VMEM(pair_row, jnp.float32),
            pltpu.VMEM(pair_row, jnp.float32),
            pltpu.VMEM(pair_row, jnp.float32),
            pltpu.VMEM(pair_row, jnp.float32),
            pltpu.VMEM(comp_row, jnp.float32),
            pltpu.VMEM(comp_row, jnp.float32),
            pltpu.VMEM((groups - 1,) + pair_row, jnp.float32),
            pltpu.VMEM((groups - 1,) + pair_row, jnp.float32),
            pltpu.VMEM((places - 1,) + comp_row, jnp.float32),
            pltpu.SemaphoreType.DMA((CHUNKS + 2,)),
            pltpu.SemaphoreType.DMA((3,)),
            pltpu.SemaphoreType.DMA((2 * (groups - 1),)),
            pltpu.SemaphoreType.DMA((2 * (groups - 1),)),
            pltpu.SemaphoreType.DMA((places - 1,)),
            pltpu.SemaphoreType.DMA((places - 1,)),
        ],
        compiler_params=pltpu.CompilerParams(
            collective_id=0, has_side_effects=True, vmem_limit_bytes=VMEM_GRANT
        ),
        name="combine",
    )(scaled, peak, total)


def write_body(scaled_hbm, factor_hbm, loglik_hbm, log_weights_hbm, out, loglik_out, log_weights_out,
               scaled, product, factor, loglik, log_weights, arrived, sent):
    comps, pairs = scaled.shape
    width = pairs // CHUNKS
    places = [pl.ds(chunk * width, width) for chunk in range(CHUNKS)]
    rows = ((factor_hbm, factor), (loglik_hbm, loglik), (log_weights_hbm, log_weights))
    loads = [pltpu.make_async_copy(there, here, arrived.at[n]) for n, (there, here) in enumerate(rows)]
    loads += [
        pltpu.make_async_copy(scaled_hbm.at[:, place], scaled.at[:, place], arrived.at[3 + n])
        for n, place in enumerate(places)
    ]
    for copy in loads:
        copy.start()
    for copy in loads[:3]:
        copy.wait()
    leaves = [
        pltpu.make_async_copy(loglik, loglik_out, sent.at[0]),
        pltpu.make_async_copy(log_weights, log_weights_out, sent.at[1]),
    ]
    for copy in leaves:
        copy.start()
    for n, place in enumerate(places):
        loads[3 + n].wait()
        product[:, place] = scaled[:, place] * factor[:, place]
        leaves.append(pltpu.make_async_copy(product.at[:, place], out.at[:, place], sent.at[2 + n]))
        leaves[-1].start()
    for copy in leaves:
        copy.wait()


def write_out(scaled, factor, loglik, log_weights):
    hbm = pl.BlockSpec(memory_space=pltpu.HBM)
    return pl.pallas_call(
        write_body,
        in_specs=[hbm] * 4,
        out_specs=[hbm] * 3,
        out_shape=[
            jax.ShapeDtypeStruct(scaled.shape, jnp.float32),
            jax.ShapeDtypeStruct(loglik.shape, jnp.float32),
            jax.ShapeDtypeStruct(log_weights.shape, jnp.float32),
        ],
        scratch_shapes=[
            pltpu.VMEM(scaled.shape, jnp.float32),
            pltpu.VMEM(scaled.shape, jnp.float32),
            pltpu.VMEM(factor.shape, jnp.float32),
            pltpu.VMEM(loglik.shape, jnp.float32),
            pltpu.VMEM(log_weights.shape, jnp.float32),
            pltpu.SemaphoreType.DMA((3 + CHUNKS,)),
            pltpu.SemaphoreType.DMA((2 + CHUNKS,)),
        ],
        compiler_params=pltpu.CompilerParams(vmem_limit_bytes=VMEM_GRANT),
        name="write_out",
    )(scaled, factor, loglik, log_weights)


def per_device(effects, se_table, se_index, base_root, grid_scale, comp_base, comp_grid, weights):
    scaled, peak, total = score_tiles(
        effects, se_table, se_index, base_root, grid_scale, comp_base, comp_grid, weights
    )
    loglik, factor, log_weights = combine(scaled, peak, total)
    responsibility, loglik, log_weights = write_out(scaled, factor, loglik, log_weights)
    return (responsibility, log_weights[0], loglik[0])


def solution(mesh):
    placed = (P(None, "pairs"), P(), P("pairs"), P(), P(), P("comp"), P("comp"), P("comp"))
    return jax.shard_map(
        per_device,
        mesh=mesh,
        in_specs=placed,
        out_specs=(P("comp", "pairs"), P("comp"), P("pairs")),
        check_vma=False,
    )
```

profile of v0, /device:TPU:0, one launch (start us, length us, event | category | flops | bytes accessed | tf_op | source)
XLA Modules:
  0.0 68.7 jit_solution(1671778486279066559)
XLA Ops:
  0.6 51.5 %score_tiles.1 = (f32[128,8192]{1,0:T(8,128)}, f32[1,8192]{1,0:T(1,128)}, f32[1,8192]{1,0:T(1,128)}) custom-call(s32[16]{0:T(128)} %index_hbm.1, f32[16,49]{1,0:T(8,128)} %se_hbm.1, f32[16]{0:T(128)} %grid_hbm.1, f32[49,8192]{1,0:T(8,128)} %effects_hbm.1, f32[49,16,49]{2,1,0:T(8,128)} %bitcast.6, s32[1,128]{1,0:T(1,128)} %bitcast.7, s32[1,128]{1,0:T(1,128)} %bitcast.8, ...), custom_call_target="tpu_custom_call" | custom-call | tf_op jit(solution)/shard_map/score_tiles/pallas_call | solution.py:275
  52.1 12.9 %combine.1 = (f32[1,8192]{1,0:T(1,128)}, f32[1,8192]{1,0:T(1,128)}, f32[1,128]{1,0:T(1,128)}) custom-call(f32[128,8192]{1,0:T(8,128)} %get-tuple-element.12.refs_0_.scaled_hbm, f32[1,8192]{1,0:T(1,128)} %get-tuple-element.13.refs_1_, f32[1,8192]{1,0:T(1,128)} %get-tuple-element.14.refs_2_), custom_call_target="tpu_custom_call" | custom-call | tf_op jit(solution)/shard_map/combine/pallas_call | solution.py:413
  65.0 3.7 %write_out.1 = (f32[128,8192]{1,0:T(8,128)}, f32[1,8192]{1,0:T(1,128)}, f32[1,128]{1,0:T(1,128)}) custom-call(f32[128,8192]{1,0:T(8,128)} %get-tuple-element.12.refs_0_.scaled_hbm, f32[1,8192]{1,0:T(1,128)} %get-tuple-element.15.factor_hbm, f32[1,8192]{1,0:T(1,128)} %get-tuple-element.16.loglik_hbm, f32[1,128]{1,0:T(1,128)} %get-tuple-element.17.log_weights_hbm), custom_call_target="tpu_custom_call" | custom-call | tf_op jit(solution)/shard_map/write_out/pallas_call | solution.py:479
where the time goes:
time: 69.7 us; the launch traced here: 68.7 us
  Pallas kernels  68 us (98%)
    pallas_call x1, Pallas kernels, score_tiles(): pl.pallas_call(score_body, in_specs=[hbm] * 8, out_specs=[hbm] * 3, scrat...  51.5 us
    pallas_call x1, Pallas kernels, combine(): pl.pallas_call(body, in_specs=[hbm] * 3, out_specs=[hbm] * 3, out_shape=[...  12.9 us
    pallas_call x1, Pallas kernels, write_out(): pl.pallas_call(write_body, in_specs=[hbm] * 4, out_specs=[hbm] * 3, out_s...  3.67 us

commit v1 on v0

--- a/solution.py
+++ b/solution.py
@@ -8,7 +8,9 @@
 from jax.sharding import PartitionSpec as P
 
 SUB = 8
-GROUP = 4
+GROUP = 2
+LN2 = math.log(2.0)
+LOG2E = 1.0 / LN2
 CHUNKS = 8
 VMEM_GRANT = 58 * 1024 * 1024
 MESH = pl.DeviceIdType.MESH
@@ -101,7 +103,7 @@
         put_row(table, core, [part * root for part in solved])
         yield
     logdet = jnp.sum(jnp.log(pivots[...]), axis=0, keepdims=True)
-    bias[...] = jnp.log(prior[...]) - 0.5 * logdet - constant
+    bias[...] = (jnp.log(prior[...]) - 0.5 * logdet - constant) * LOG2E
 
 
 def pack_tile(tile, effects, wide, ready):
@@ -120,9 +122,9 @@
     columns = pl.ds(pl.multiple_of(tile * width, width), width)
     values = found[...].T
     top = jnp.max(values, axis=0, keepdims=True)
-    shifted = jnp.exp(values - top)
+    shifted = jnp.exp2(values - top)
     scaled[:, columns] = shifted
-    peak[:, columns] = top
+    peak[:, columns] = top * LN2
     total[:, columns] = jnp.sum(shifted, axis=0, keepdims=True)
 
 
@@ -143,7 +145,7 @@
         elif index < last:
             quad[...] += part
         else:
-            found[...] = bias[...] - 0.5 * (quad[...] + part)
+            found[...] = bias[...] - (0.5 * LOG2E) * (quad[...] + part)
         if index % (GROUP // 2) == GROUP // 2 - 1:
             yield
 

time: 69.7 us -> 69.6 us (level); the launches traced: 68.7 us -> 70.3 us
  Pallas kernels: 68 us -> 69.6 us
    pallas_call x1, Pallas kernels: 12.9 us -> 14.4 us  [combine(): pl.pallas_call(body, in_specs=[hbm] * 3, out_specs=[hbm] * 3, out_shape=[...]
where the time goes in v1:
time: 69.6 us; the launch traced here: 70.3 us
  Pallas kernels  69.6 us (100%)
    pallas_call x1, Pallas kernels, score_tiles(): pl.pallas_call(score_body, in_specs=[hbm] * 8, out_specs=[hbm] * 3, scrat...  51.5 us
    pallas_call x1, Pallas kernels, combine(): pl.pallas_call(body, in_specs=[hbm] * 3, out_specs=[hbm] * 3, out_shape=[...  14.4 us
    pallas_call x1, Pallas kernels, write_out(): pl.pallas_call(write_body, in_specs=[hbm] * 4, out_specs=[hbm] * 3, out_s...  3.67 us

profile of v1, /device:TPU:0, one launch (start us, length us, event | category | flops | bytes accessed | tf_op | source)
XLA Modules:
  0.0 70.3 jit_solution(4263864636118173231)
XLA Ops:
  0.6 51.5 %score_tiles.1 = (f32[128,8192]{1,0:T(8,128)}, f32[1,8192]{1,0:T(1,128)}, f32[1,8192]{1,0:T(1,128)}) custom-call(s32[16]{0:T(128)} %index_hbm.1, f32[16,49]{1,0:T(8,128)} %se_hbm.1, f32[16]{0:T(128)} %grid_hbm.1, f32[49,8192]{1,0:T(8,128)} %effects_hbm.1, f32[49,16,49]{2,1,0:T(8,128)} %bitcast.6, s32[1,128]{1,0:T(1,128)} %bitcast.7, s32[1,128]{1,0:T(1,128)} %bitcast.8, ...), custom_call_target="tpu_custom_call" | custom-call | tf_op jit(solution)/shard_map/score_tiles/pallas_call | solution.py:277
  52.1 14.4 %combine.1 = (f32[1,8192]{1,0:T(1,128)}, f32[1,8192]{1,0:T(1,128)}, f32[1,128]{1,0:T(1,128)}) custom-call(f32[128,8192]{1,0:T(8,128)} %get-tuple-element.12.refs_0_.scaled_hbm, f32[1,8192]{1,0:T(1,128)} %get-tuple-element.13.refs_1_, f32[1,8192]{1,0:T(1,128)} %get-tuple-element.14.refs_2_), custom_call_target="tpu_custom_call" | custom-call | tf_op jit(solution)/shard_map/combine/pallas_call | solution.py:415
  66.6 3.7 %write_out.1 = (f32[128,8192]{1,0:T(8,128)}, f32[1,8192]{1,0:T(1,128)}, f32[1,128]{1,0:T(1,128)}) custom-call(f32[128,8192]{1,0:T(8,128)} %get-tuple-element.12.refs_0_.scaled_hbm, f32[1,8192]{1,0:T(1,128)} %get-tuple-element.15.factor_hbm, f32[1,8192]{1,0:T(1,128)} %get-tuple-element.16.loglik_hbm, f32[1,128]{1,0:T(1,128)} %get-tuple-element.17.log_weights_hbm), custom_call_target="tpu_custom_call" | custom-call | tf_op jit(solution)/shard_map/write_out/pallas_call | solution.py:481
